TPU v7x, 32 devices: a whole 2x2x4 slice. The times are simulated.
32 devices in a mesh: groups: 2 (over y), seq: 4 (over z), heads: 2 (over x), sub: 2 (over core).
Axes of the slice: x: 2, y: 2, z: 4, core: 2. Of those that a mesh axis runs over, the one named last changes fastest.
Arguments:
- queries: bfloat16 [2048, 8192], P(('groups', 'seq', 'sub'), 'heads'), parts along dimension 0, may hold values from -400 to 400
- keys: bfloat16 [2048, 1024], P(('groups', 'seq', 'sub'), 'heads'), parts along dimension 0, may hold values from -6 to 6
- values: bfloat16 [2048, 1024], P(('groups', 'seq', 'sub'), 'heads'), parts along dimension 0, may hold values from -18 to 18
- half_order: int32 [32], P('groups'), parts along dimension 0, may hold values from 0 to 15, as said below
- frame_lengths: int32 [16], P('groups'), parts along dimension 0, may hold values from 1 to 256, 1024 in all
- out_proj: bfloat16 [8192, 4096], P('heads', ('seq', 'sub')), may hold values from -0.09375 to 0.09375
- residual_in: bfloat16 [2048, 4096], P(('groups', 'seq', 'sub'), 'heads'), parts along dimension 0, may hold values from -40 to 40
- norm_gain: float32 [4096], P('heads'), may hold values from 0.5 to 1.5
Outputs:
- attended: bfloat16 [2048, 8192], P(('groups', 'seq', 'sub'), 'heads'), parts along dimension 0
- hidden_state: bfloat16 [2048, 4096], P(('groups', 'seq', 'sub'), 'heads'), parts along dimension 0
- normed: bfloat16 [2048, 4096], P(('groups', 'seq', 'sub'), 'heads'), parts along dimension 0
There are 2 independent parts, one for each index of `groups`. A program takes and returns all parts, laid end to end along the dimension named above; an argument that names none is the same for every part. Nothing has to cross between parts.
Inputs may be any that keep to these rules, and one draw needn't show every extreme that they name: `half_order`: a permutation of 0 to 15.
All inputs are finite; a program needn't handle non-finite values.
Results may differ from a plain program's by a relative error of at most 0.005.
Values may be sent and summed in bfloat16 or wider, within the bound.
A program may use at most 128 MiB of HBM per device.

v0:
```python
import jax
import jax.numpy as jnp
from jax import lax
from jax.sharding import PartitionSpec as P

HEAD_WIDTH = 128
OUT_WIDTH = 4096


def shards(queries, keys, values, half_order, frame_lengths, out_proj, residual_in, norm_gain):
    tok_rows = queries.shape[0]
    kv_local = keys.shape[1] // HEAD_WIDTH
    group_width = queries.shape[1] // keys.shape[1]
    half_rows = tok_rows // 2
    own_index = lax.axis_index("seq") * lax.axis_size("sub") + lax.axis_index("sub")
    table_ids = jnp.arange(half_order.shape[0], dtype=jnp.int32)

    def locate(row_ids):
        matches = (row_ids // half_rows)[:, None] == table_ids[None, :]
        offsets = jnp.sum(jnp.where(matches, half_order[None, :], 0), axis=1)
        return offsets * half_rows + row_ids % half_rows

    query_pos = locate(own_index * tok_rows + jnp.arange(tok_rows, dtype=jnp.int32))
    frame_ends = jnp.cumsum(frame_lengths)
    frame_starts = frame_ends - frame_lengths
    frame_limit = jnp.sum(
        jnp.where(frame_starts[None, :] <= query_pos[:, None], frame_lengths[None, :], 0), axis=1
    )
    query_head_rows = queries.reshape(tok_rows, kv_local, group_width, HEAD_WIDTH)
    score_scale = HEAD_WIDTH ** (-0.5)
    initial = (
        jnp.full((kv_local, group_width, tok_rows), -1e30, jnp.float32),
        jnp.zeros((kv_local, group_width, tok_rows), jnp.float32),
        jnp.zeros((kv_local, group_width, tok_rows, HEAD_WIDTH), jnp.float32),
    )
    key_piece = lax.all_gather(keys, ("seq", "sub"), axis=0, tiled=True)
    value_piece = lax.all_gather(values, ("seq", "sub"), axis=0, tiled=True)
    piece_rows = key_piece.shape[0]
    key_pos = locate(jnp.arange(piece_rows, dtype=jnp.int32))

    def absorb_piece(current):
        running_max, denominator, numerator = current
        key_view = key_piece.reshape(piece_rows, kv_local, HEAD_WIDTH)
        value_view = value_piece.reshape(piece_rows, kv_local, HEAD_WIDTH)
        scores = (
            jnp.einsum(
                "qhgd,khd->hgqk", query_head_rows, key_view, preferred_element_type=jnp.float32
            )
            * score_scale
        )
        visible = key_pos[None, :] < frame_limit[:, None]
        scores = jnp.where(visible, scores, -1e30)
        new_max = jnp.maximum(running_max, jnp.max(scores, axis=-1))
        weights = jnp.where(visible, jnp.exp(scores - new_max[..., None]), 0.0)
        denominator = jnp.sum(weights, axis=-1)
        product = jnp.einsum(
            "hgqk,khd->hgqd",
            weights.astype(jnp.bfloat16),
            value_view,
            preferred_element_type=jnp.float32,
        )
        numerator = product
        return (new_max, denominator, numerator)

    running_max, denominator, numerator = lax.cond(
        jnp.min(key_pos) < jnp.max(frame_limit), absorb_piece, lambda current: current, initial
    )
    result = numerator / denominator[..., None]
    attended = (
        jnp.transpose(result, (2, 0, 1, 3))
        .reshape(tok_rows, kv_local * group_width * HEAD_WIDTH)
        .astype(jnp.bfloat16)
    )
    head_terms = jnp.dot(
        attended,
        lax.all_gather(out_proj, ("seq", "sub"), axis=1, tiled=True),
        preferred_element_type=jnp.float32,
    )
    projected = lax.psum_scatter(
        head_terms.astype(jnp.bfloat16), "heads", scatter_dimension=1, tiled=True
    ).astype(jnp.float32)
    hidden_state = (residual_in.astype(jnp.float32) + projected).astype(jnp.bfloat16)
    widened = hidden_state.astype(jnp.float32)
    energy = lax.psum(jnp.sum(widened * widened, axis=1), "heads") / OUT_WIDTH
    normed = (widened * lax.rsqrt(energy + 1e-06)[:, None] * norm_gain[None, :]).astype(
        jnp.bfloat16
    )
    return (attended, hidden_state, normed)


def solution(mesh):
    in_specs = (
        P(("groups", "seq", "sub"), "heads"),
        P(("groups", "seq", "sub"), "heads"),
        P(("groups", "seq", "sub"), "heads"),
        P("groups"),
        P("groups"),
        P("heads", ("seq", "sub")),
        P(("groups", "seq", "sub"), "heads"),
        P("heads"),
    )
    out_specs = (
        P(("groups", "seq", "sub"), "heads"),
        P(("groups", "seq", "sub"), "heads"),
        P(("groups", "seq", "sub"), "heads"),
    )
    return jax.shard_map(shards, mesh=mesh, in_specs=in_specs, out_specs=out_specs, check_vma=False)
```

profile of v0, /device:TPU:1, one launch (start us, length us, event | category | flops | bytes accessed | tf_op | source)
XLA Modules:
  0.0 392.5 jit_solution(6469094071069195550)
XLA Ops:
  7.2 0.7 all-gather.4.cloned.1.call-update
  7.9 0.0 all-gather.6.cloned.1.call-start
  7.9 0.7 all-gather.6.cloned.1.call-update
  8.6 0.0 all-gather.8.cloned.1.call-start
  8.7 0.7 all-gather.8.cloned.1.call-update
  9.4 0.0 reduce-scatter.2.cloned.1.call-start
  9.4 0.8 reduce-window.9
  10.3 0.7 select_reduce_fusion.1
  11.0 0.7 bitcast_subtract_fusion
  11.7 0.7 select_reduce_fusion.2
  12.4 0.6 reduce_max.18
  13.1 0.7 select_reduce_fusion
  13.8 0.6 fusion.26
  15.8 18.5 %all-gather.4.cloned.1.call-done = bf16[1024,512]{1,0:T(8,128)(2,1)} async-done(((bf16[128,512]{1,0:T(8,128)(2,1)}), bf16[1024,512]{1,0:T(8,128)(2,1)}) %all-gather.4.cloned.1.call-update) | async-done | bytes 1048592 | tf_op jit(solution)/shard_map/all_gather | solution.py:36
  34.3 23.5 %all-gather.6.cloned.1.call-done = bf16[1024,512]{1,0:T(8,128)(2,1)} async-done(((bf16[128,512]{1,0:T(8,128)(2,1)}), bf16[1024,512]{1,0:T(8,128)(2,1)}) %all-gather.6.cloned.1.call-update) | async-done | bytes 1048592 | tf_op jit(solution)/shard_map/all_gather | solution.py:37
  57.8 32.1 %conditional.1 = (f32[4,8,128]{2,1,0:T(8,128)S(1)}, f32[4,8,128,128]{3,2,1,0:T(8,128)S(1)}) conditional(s32[]{:T(128)} %convert_element_type.33, () %tuple.16, (s32[1024]{0:T(1024)S(1)}, s32[128]{0:T(128)S(1)}, bf16[1024,512]{1,0:T(8,128)(2,1)}, bf16[128,4096]{1,0:T(8,128)(2,1)}, bf16[1024,512]{1,0:T(8,128)(2,1)}) %tuple.17), branch_computations={%region_6.7_spmd, %region_7.10_spmd} | conditional | flops 2202136576 | bytes 66687532 | solution.py:65
  57.8 0.2 broadcast_compare_fusion
  58.0 1.4 reshape.99
  59.4 1.5 copy.29
  60.9 8.6 %fusion = (f32[4,8,128]{2,1,0:T(8,128)S(1)}, f32[4,1024,128,8]{2,1,3,0:T(8,128)}) fusion(pred[128,1024]{0,1:T(8,128)(4,1)S(1)} %broadcast_compare_fusion, bf16[128,4,8,128]{3,2,1,0:T(8,128)(2,1)S(1)} %bitcast.32, bf16[1024,4,128,1]{2,1,0,3:T(4,128)(2,1)S(1)} %bitcast.31), kind=kOutput, calls=%fused_computation.2 | convolution fusion | flops 1086320640 | bytes 19021824 | tf_op jit(solution)/shard_map/cond/branch_1_fun/qhgd,khd->hgqk/dot_general | solution.py:46
  69.5 0.3 reshape.101
  69.7 12.1 %fusion.3 = f32[4,8,128,128]{3,2,1,0:T(8,128)S(1)} fusion(f32[4,1024,128,8]{2,1,3,0:T(8,128)} %get-tuple-element.30, f32[4,8,128]{2,1,0:T(8,128)S(1)} %broadcast_maximum_fusion, pred[128,1024]{0,1:T(8,128)(4,1)S(1)} %broadcast_compare_fusion, bf16[1024,4,128,1]{2,1,0,3:T(4,128)(2,1)S(1)} %bitcast.34), kind=kOutput, calls=%fused_computation.5 | convolution fusion | flops 1094713344 | bytes 20070400 | tf_op jit(solution)/shard_map/cond/branch_1_fun/hgqk,khd->hgqd/dot_general | solution.py:56
  81.8 8.1 %fusion.2 = f32[4,8,128]{2,1,0:T(8,128)S(1)} fusion(f32[4,1024,128,8]{2,1,3,0:T(8,128)} %get-tuple-element.30, f32[4,8,128]{2,1,0:T(8,128)S(1)} %broadcast_maximum_fusion, pred[128,1024]{0,1:T(8,128)(4,1)S(1)} %broadcast_compare_fusion), kind=kLoop, calls=%fused_computation.4 | loop fusion | flops 20967424 | bytes 16941056 | tf_op jit(solution)/shard_map/cond/branch_1_fun/reduce_sum | solution.py:55
  89.9 0.7 fusion.16
  90.6 0.7 copy.21
  91.3 0.5 copy.42
  91.8 255.9 %all-gather.8.cloned.1.call-done = bf16[4096,4096]{1,0:T(8,128)(2,1)} async-done(((bf16[4096,512]{1,0:T(8,128)(2,1)}), bf16[4096,4096]{1,0:T(8,128)(2,1)}) %all-gather.8.cloned.1.call-update) | async-done | bytes 33554448 | tf_op jit(solution)/shard_map/all_gather | solution.py:76
  347.7 14.1 %convolution_convert_fusion = bf16[128,4096]{1,0:T(8,128)(2,1)} fusion(bf16[128,4096]{1,0:T(8,128)(2,1)S(1)} %bitcast.28, bf16[4096,4096]{1,0:T(8,128)(2,1)} %all-gather.8.cloned.1.call-done), kind=kOutput, calls=%fused_computation.16 | convolution fusion | flops 4295491584 | bytes 35651584 | tf_op jit(solution)/shard_map/dot_general | solution.py:74
  361.8 18.2 %reduce-scatter.2.cloned.1.call-done = bf16[128,2048]{1,0:T(8,128)(2,1)} async-done(((bf16[128,4096]{1,0:T(8,128)(2,1)}), bf16[128,2048]{1,0:T(8,128)(2,1)}) %reduce-scatter.2.cloned.1.call-update) | async-done | bytes 524304 | tf_op jit(solution)/shard_map/reduce_scatter | solution.py:79
  379.9 1.3 fusion.13
  381.2 3.8 psum.7
  385.0 1.0 fusion.15
  (17 shorter events, 0.1 us)
Async XLA Ops:
  7.2 27.1 %all-gather.4.cloned.1.call-start = ((), (), s32[]{:S(2)}) async-start(), calls=%async_computation.1 | async-start | bytes 1179648 | tf_op jit(solution)/shard_map/all_gather | solution.py:36
  7.9 49.9 %all-gather.6.cloned.1.call-start = ((), (), s32[]{:S(2)}) async-start(), calls=%async_computation.2 | async-start | bytes 1179648 | tf_op jit(solution)/shard_map/all_gather | solution.py:37
  8.6 339.0 %all-gather.8.cloned.1.call-start = ((), (), s32[]{:S(2)}) async-start(), calls=%async_computation.3 | async-start | bytes 37748736 | tf_op jit(solution)/shard_map/all_gather | solution.py:76
  9.4 370.5 %reduce-scatter.2.cloned.1.call-start = ((), (), s32[]{:S(2)}) async-start(), calls=%async_computation.4 | async-start | bytes 1572864 | tf_op jit(solution)/shard_map/reduce_scatter | solution.py:79
  57.8 11.7 %copy-start.2 = (bf16[1024,512]{1,0:T(8,128)(2,1)S(1)}, bf16[1024,512]{1,0:T(8,128)(2,1)}, u32[]{:S(2)}) copy-start(bf16[1024,512]{1,0:T(8,128)(2,1)} %get-tuple-element.15) | copy-start | bytes 3145732 | tf_op jit(solution)/shard_map/cond
  91.8 270.0 %copy-start = (bf16[16,8,32,128]{3,1,2,0:T(8,128)(2,1)}, bf16[16,8,32,128]{3,1,2,0:T(8,128)(2,1)S(1)}, u32[]{:S(2)}) copy-start(bf16[16,8,32,128]{3,1,2,0:T(8,128)(2,1)S(1)} %copy.42) | copy-start | bytes 3145732
  347.7 32.3 %copy-start.3 = (bf16[128,2048]{1,0:T(8,128)(2,1)S(1)}, bf16[128,2048]{1,0:T(8,128)(2,1)}, u32[]{:S(2)}) copy-start(bf16[128,2048]{1,0:T(8,128)(2,1)} %param.16) | copy-start | bytes 1572868
  347.7 37.4 %copy-start.4 = (f32[2048]{0:T(1024)S(1)}, f32[2048]{0:T(1024)}, u32[]{:S(2)}) copy-start(f32[2048]{0:T(1024)} %param.17) | copy-start | bytes 24580
  381.2 4.8 %copy-start.1 = (bf16[128,2048]{1,0:T(8,128)(2,1)}, bf16[128,2048]{1,0:T(8,128)(2,1)S(1)}, u32[]{:S(2)}) copy-start(bf16[128,2048]{1,0:T(8,128)(2,1)S(1)} %get-tuple-element.26) | copy-start | bytes 1572868
Sparse Core Ops, SparseCore 0:
  9.6 24.6 all-gather.3
  35.9 21.8 all-gather.5
  59.4 288.2 all-gather.7
  361.9 17.9 reduce-scatter.1
where the time goes:
time: 395 us; the launch traced here: 393 us
  waiting for transfers between devices  318 us (81%)
  matrix products  34.7 us (9%)
  other arithmetic  16.3 us (4%)
  between operations  15.1 us (4%)
  local copies, waits for them, and re-layouts  4.32 us (1%)
    all_gather x1, waiting for transfers between devices, shards(): lax.all_gather(out_proj, ('seq', 'sub'), axis=1, tiled=True)  256 us
    all_gather x1, waiting for transfers between devices, shards(): value_piece = lax.all_gather(values, ('seq', 'sub'), axis=0, tiled=True)  23.5 us
    all_gather x1, waiting for transfers between devices, shards(): key_piece = lax.all_gather(keys, ('seq', 'sub'), axis=0, tiled=True)  18.5 us
    reduce_scatter x1, waiting for transfers between devices, shards(): lax.psum_scatter(head_terms.astype(jnp.bfloat16), 'heads', scatter_dimens...  18.2 us
    dot_general x1, matrix products, shards(): jnp.dot(attended, lax.all_gather(out_proj, ('seq', 'sub'), axis=1, tiled=...  14.1 us
    dot_general x1, matrix products, absorb_piece(): jnp.einsum('hgqk,khd->hgqd', weights.astype(jnp.bfloat16), value_view, pr...  12.1 us
    dot_general x1, matrix products, absorb_piece(): jnp.einsum('qhgd,khd->hgqk', query_head_rows, key_view, preferred_element...  8.55 us
    reduce_sum x1, other arithmetic, absorb_piece(): denominator = jnp.sum(weights, axis=-1)  8.06 us
  transfers between devices with their start and end apart: 4, of which 4 were waited for; matrix products, arithmetic and copies ran while one was open for 10% of the time, Pallas kernels for 0%

commit v1 on v0

--- a/solution.py
+++ b/solution.py
@@ -71,13 +71,13 @@
         .reshape(tok_rows, kv_local * group_width * HEAD_WIDTH)
         .astype(jnp.bfloat16)
     )
-    head_terms = jnp.dot(
-        attended,
-        lax.all_gather(out_proj, ("seq", "sub"), axis=1, tiled=True),
-        preferred_element_type=jnp.float32,
+    gathered = lax.all_gather(attended, ("seq", "sub"), axis=0, tiled=True)
+    column_terms = jnp.dot(gathered, out_proj, preferred_element_type=jnp.float32)
+    head_terms = lax.all_to_all(
+        column_terms.astype(jnp.bfloat16), ("seq", "sub"), split_axis=0, concat_axis=1, tiled=True
     )
     projected = lax.psum_scatter(
-        head_terms.astype(jnp.bfloat16), "heads", scatter_dimension=1, tiled=True
+        head_terms, "heads", scatter_dimension=1, tiled=True
     ).astype(jnp.float32)
     hidden_state = (residual_in.astype(jnp.float32) + projected).astype(jnp.bfloat16)
     widened = hidden_state.astype(jnp.float32)

time: 395 us -> 243 us (0.62)
  waiting for transfers between devices: 318 us -> 145 us
  blocking collectives: 3.78 us -> 32 us
  matrix products: 34.7 us -> 25.3 us
    all_gather x1, waiting for transfers between devices: 256 us -> 81.7 us  [shards(): gathered = lax.all_gather(attended, ('seq', 'sub'), axis=0, tiled=True)]
    all_to_all x0 -> x1, blocking collectives: none -> 28.2 us  [shards(): lax.all_to_all(column_terms.astype(jnp.bfloat16), ('seq', 'sub'), split_a...]
    dot_general x1, matrix products: 14.1 us -> 9.06 us  [shards(): jnp.dot(gathered, out_proj, preferred_element_type=jnp.float32)]
  transfers between devices with their start and end apart: 4 -> 4, of which waited for: 4 -> 4; matrix products, arithmetic and copies ran while one was open for 10% -> 2% of each run, Pallas kernels for 0% -> 0%
where the time goes in v1:
time: 243 us; the launch traced here: 241 us
  waiting for transfers between devices  145 us (60%)
  blocking collectives  32 us (13%)
  matrix products  25.3 us (10%)
  other arithmetic  16.2 us (7%)
  between operations  15.1 us (6%)
  local copies, waits for them, and re-layouts  6.39 us (3%)
    all_gather x1, waiting for transfers between devices, shards(): gathered = lax.all_gather(attended, ('seq', 'sub'), axis=0, tiled=True)  81.7 us
    all_to_all x1, blocking collectives, shards(): lax.all_to_all(column_terms.astype(jnp.bfloat16), ('seq', 'sub'), split_a...  28.2 us
    all_gather x1, waiting for transfers between devices, shards(): value_piece = lax.all_gather(values, ('seq', 'sub'), axis=0, tiled=True)  23.5 us
    reduce_scatter x1, waiting for transfers between devices, shards(): lax.psum_scatter(head_terms, 'heads', scatter_dimension=1, tiled=True)  19.6 us
    all_gather x1, waiting for transfers between devices, shards(): key_piece = lax.all_gather(keys, ('seq', 'sub'), axis=0, tiled=True)  19.3 us
    dot_general x1, matrix products, shards(): jnp.dot(gathered, out_proj, preferred_element_type=jnp.float32)  9.06 us
    dot_general x1, matrix products, absorb_piece(): jnp.einsum('hgqk,khd->hgqd', weights.astype(jnp.bfloat16), value_view, pr...  8.97 us
    reduce_sum x1, other arithmetic, absorb_piece(): denominator = jnp.sum(weights, axis=-1)  7.98 us
  transfers between devices with their start and end apart: 4, of which 4 were waited for; matrix products, arithmetic and copies ran while one was open for 2% of the time, Pallas kernels for 0%

profile of v1, /device:TPU:1, one launch (start us, length us, event | category | flops | bytes accessed | tf_op | source)
XLA Modules:
  0.0 240.7 jit_solution(11686447598363568925)
XLA Ops:
  7.2 0.7 all-gather.4.cloned.1.call-update
  7.9 0.7 all-gather.6.cloned.1.call-update
  8.6 0.0 all-gather.8.cloned.1.call-start
  8.7 0.8 reduce-window.9
  9.5 0.7 select_reduce_fusion.1
  10.3 0.7 bitcast_subtract_fusion
  11.0 0.7 select_reduce_fusion.2
  11.7 0.6 reduce_max.18
  12.3 0.7 select_reduce_fusion
  13.1 0.6 fusion.26
  15.0 19.3 %all-gather.4.cloned.1.call-done = bf16[1024,512]{1,0:T(8,128)(2,1)} async-done(((bf16[128,512]{1,0:T(8,128)(2,1)}), bf16[1024,512]{1,0:T(8,128)(2,1)}) %all-gather.4.cloned.1.call-update) | async-done | bytes 1048592 | tf_op jit(solution)/shard_map/all_gather | solution.py:36
  34.3 23.5 %all-gather.6.cloned.1.call-done = bf16[1024,512]{1,0:T(8,128)(2,1)} async-done(((bf16[128,512]{1,0:T(8,128)(2,1)}), bf16[1024,512]{1,0:T(8,128)(2,1)}) %all-gather.6.cloned.1.call-update) | async-done | bytes 1048592 | tf_op jit(solution)/shard_map/all_gather | solution.py:37
  57.8 27.6 %conditional.1 = (f32[4,8,128]{2,1,0:T(8,128)S(1)}, f32[4,8,128,128]{3,2,1,0:T(8,128)S(1)}) conditional(s32[]{:T(128)} %convert_element_type.33, () %tuple.16, (s32[1024]{0:T(1024)S(1)}, s32[128]{0:T(128)S(1)}, bf16[1024,512]{1,0:T(8,128)(2,1)}, bf16[128,4096]{1,0:T(8,128)(2,1)}, bf16[1024,512]{1,0:T(8,128)(2,1)}) %tuple.17), branch_computations={%region_6.7_spmd, %region_7.10_spmd} | conditional | flops 2202136576 | bytes 66687532 | solution.py:65
  57.8 0.2 broadcast_compare_fusion
  58.0 1.4 reshape.102
  59.4 1.5 copy.31
  60.9 7.2 %fusion = (f32[4,8,128]{2,1,0:T(8,128)S(1)}, f32[4,1024,128,8]{2,1,3,0:T(8,128)}) fusion(pred[128,1024]{0,1:T(8,128)(4,1)S(1)} %broadcast_compare_fusion, bf16[128,4,8,128]{3,2,1,0:T(8,128)(2,1)S(1)} %bitcast.38, bf16[1024,4,128,1]{2,1,0,3:T(4,128)(2,1)S(1)} %bitcast.37), kind=kOutput, calls=%fused_computation.2 | convolution fusion | flops 1086320640 | bytes 19021824 | tf_op jit(solution)/shard_map/cond/branch_1_fun/qhgd,khd->hgqk/dot_general | solution.py:46
  68.1 0.3 reshape.104
  68.4 9.0 %fusion.3 = f32[4,8,128,128]{3,2,1,0:T(8,128)S(1)} fusion(f32[4,1024,128,8]{2,1,3,0:T(8,128)} %get-tuple-element.30, f32[4,8,128]{2,1,0:T(8,128)S(1)} %broadcast_maximum_fusion, pred[128,1024]{0,1:T(8,128)(4,1)S(1)} %broadcast_compare_fusion, bf16[1024,4,128,1]{2,1,0,3:T(4,128)(2,1)S(1)} %bitcast.41), kind=kOutput, calls=%fused_computation.5 | convolution fusion | flops 1094713344 | bytes 20070400 | tf_op jit(solution)/shard_map/cond/branch_1_fun/hgqk,khd->hgqd/dot_general | solution.py:56
  77.4 8.0 %fusion.2 = f32[4,8,128]{2,1,0:T(8,128)S(1)} fusion(f32[4,1024,128,8]{2,1,3,0:T(8,128)} %get-tuple-element.30, f32[4,8,128]{2,1,0:T(8,128)S(1)} %broadcast_maximum_fusion, pred[128,1024]{0,1:T(8,128)(4,1)S(1)} %broadcast_compare_fusion), kind=kLoop, calls=%fused_computation.4 | loop fusion | flops 20967424 | bytes 16941056 | tf_op jit(solution)/shard_map/cond/branch_1_fun/reduce_sum | solution.py:55
  85.4 0.7 fusion.16
  86.1 0.7 copy.22
  86.8 1.4 copy.45
  88.3 0.0 reduce-scatter.2.cloned.1.call-start
  88.3 81.7 %all-gather.8.cloned.1.call-done = bf16[1024,4096]{1,0:T(8,128)(2,1)} async-done(((bf16[128,4096]{1,0:T(8,128)(2,1)}), bf16[1024,4096]{1,0:T(8,128)(2,1)}) %all-gather.8.cloned.1.call-update) | async-done | bytes 8388624 | tf_op jit(solution)/shard_map/all_gather | solution.py:74
  170.0 9.1 %convolution_convert_fusion = bf16[1024,512]{1,0:T(8,128)(2,1)S(1)} fusion(bf16[1024,4096]{1,0:T(8,128)(2,1)} %all-gather.8.cloned.1.call-done, bf16[4096,512]{1,0:T(8,128)(2,1)} %param.15), kind=kOutput, calls=%fused_computation.17 | convolution fusion | flops 4295491584 | bytes 13631488 | tf_op jit(solution)/shard_map/dot_general | solution.py:75
  179.1 28.2 %all_to_all.19 = bf16[8,128,512]{2,1,0:T(8,128)(2,1)S(1)} all-to-all(bf16[8,128,512]{2,1,0:T(8,128)(2,1)S(1)} %bitcast.40), channel_id=1, replica_groups=mesh['groups'=2,'seq'=4,'heads'=2,'sub'=2] {'seq','sub'}, dimensions={0} | all-to-all | bytes 2097152 | tf_op jit(solution)/shard_map/all_to_all | solution.py:76
  207.3 1.1 copy.32
  208.4 19.6 %reduce-scatter.2.cloned.1.call-done = bf16[128,2048]{1,0:T(8,128)(2,1)} async-done(((bf16[128,4096]{1,0:T(8,128)(2,1)}), bf16[128,2048]{1,0:T(8,128)(2,1)}) %reduce-scatter.2.cloned.1.call-update) | async-done | bytes 524304 | tf_op jit(solution)/shard_map/reduce_scatter | solution.py:79
  228.0 1.3 fusion.13
  229.3 3.8 %psum.7 = f32[128]{0:T(128)S(1)} all-reduce(f32[128]{0:T(128)S(1)} %get-tuple-element.25), channel_id=1, replica_groups=mesh['groups'=2,'seq'=4,'heads'=2,'sub'=2] {'heads'}, use_global_device_ids=true, to_apply=%region_12.13 | all-reduce | flops 128 | bytes 1024 | tf_op jit(solution)/shard_map/psum | solution.py:84
  233.1 1.0 fusion.15
  (17 shorter events, 0.2 us)
Async XLA Ops:
  7.2 27.1 %all-gather.4.cloned.1.call-start = ((), (), s32[]{:S(2)}) async-start(), calls=%async_computation.2 | async-start | bytes 1179648 | tf_op jit(solution)/shard_map/all_gather | solution.py:36
  7.9 49.9 %all-gather.6.cloned.1.call-start = ((), (), s32[]{:S(2)}) async-start(), calls=%async_computation.3 | async-start | bytes 1179648 | tf_op jit(solution)/shard_map/all_gather | solution.py:37
  8.6 161.4 %all-gather.8.cloned.1.call-start = ((), (), s32[]{:S(2)}) async-start(), calls=%async_computation.4 | async-start | bytes 9437184 | tf_op jit(solution)/shard_map/all_gather | solution.py:74
  57.8 10.4 %copy-start.1 = (bf16[1024,512]{1,0:T(8,128)(2,1)S(1)}, bf16[1024,512]{1,0:T(8,128)(2,1)}, u32[]{:S(2)}) copy-start(bf16[1024,512]{1,0:T(8,128)(2,1)} %get-tuple-element.15) | copy-start | bytes 3145732 | tf_op jit(solution)/shard_map/cond
  88.2 139.8 %copy-start.2 = (bf16[128,2048]{1,0:T(8,128)(2,1)S(1)}, bf16[128,2048]{1,0:T(8,128)(2,1)}, u32[]{:S(2)}) copy-start(bf16[128,2048]{1,0:T(8,128)(2,1)} %param.16) | copy-start | bytes 1572868
  88.2 144.9 %copy-start.3 = (f32[2048]{0:T(1024)S(1)}, f32[2048]{0:T(1024)}, u32[]{:S(2)}) copy-start(f32[2048]{0:T(1024)} %param.17) | copy-start | bytes 24580
  88.3 139.8 %reduce-scatter.2.cloned.1.call-start = ((), (), s32[]{:S(2)}) async-start(), calls=%async_computation.5 | async-start | bytes 1572864 | tf_op jit(solution)/shard_map/reduce_scatter | solution.py:79
  229.3 4.8 %copy-start = (bf16[128,2048]{1,0:T(8,128)(2,1)}, bf16[128,2048]{1,0:T(8,128)(2,1)S(1)}, u32[]{:S(2)}) copy-start(bf16[128,2048]{1,0:T(8,128)(2,1)S(1)} %get-tuple-element.26) | copy-start | bytes 1572868
Sparse Core Ops, SparseCore 0:
  9.6 24.6 all-gather.3
  35.9 21.8 all-gather.5
  88.4 81.6 all-gather.7
  208.6 19.4 reduce-scatter.1

commit v2 on v1

v2 whole, which is shorter than its diff:
```python
import functools
import math

import jax
import jax.numpy as jnp
from jax import lax
from jax.experimental import pallas as pl
from jax.experimental.pallas import tpu as pltpu
from jax.sharding import PartitionSpec as P

HEAD_WIDTH = 128
MESH = pl.DeviceIdType.MESH


def kernel(dims, order_ref, frames_ref, q_ref, kv_ref, proj_hbm, res_ref, gain_ref,
           att_out, hidden_out, normed_out,
           kvbuf, attbuf, proj, bias, acc, pbuf, retbuf, ebuf,
           proj_sem, kv_send, kv_recv, at_send, at_recv, ret_send, ret_recv, en_send, en_recv):
    S, C, H, G = dims
    n = S * C
    blocks = n // H
    rows = q_ref.shape[0]
    width = q_ref.shape[1] // G
    cols = proj.shape[1]
    total = n * rows
    z, c, h = lax.axis_index("seq"), lax.axis_index("sub"), lax.axis_index("heads")
    own = z * C + c
    home = own // blocks
    home_slot = own % blocks

    proj_copy = pltpu.make_async_copy(proj_hbm, proj, proj_sem)
    proj_copy.start()

    barrier = pltpu.get_barrier_semaphore()

    def greet(t, carry):
        other = lax.rem(own * H + h + t, n * H)
        place = other // H
        pl.semaphore_signal(
            barrier, inc=1,
            device_id={"seq": place // C, "sub": place % C, "heads": other % H},
            device_id_type=MESH,
        )
        return carry

    lax.fori_loop(1, n * H, greet, 0)

    half_rows = total // order_ref.shape[0]
    per_device = rows // half_rows
    lane = lax.broadcasted_iota(jnp.int32, (1, total), 1)
    key_pos = jnp.zeros((1, total), jnp.int32)
    for t in range(order_ref.shape[0]):
        inside = (lane >= t * half_rows) & (lane < (t + 1) * half_rows)
        key_pos = jnp.where(inside, lane + (order_ref[t] - t) * half_rows, key_pos)
    line = lax.broadcasted_iota(jnp.int32, (rows, 1), 0)
    row_pos = jnp.zeros((rows, 1), jnp.int32)
    for t in range(per_device):
        inside = (line >= t * half_rows) & (line < (t + 1) * half_rows)
        row_pos = jnp.where(inside, line + (order_ref[own * per_device + t] - t) * half_rows, row_pos)
    limit = jnp.zeros((rows, 1), jnp.int32)
    first = jnp.int32(0)
    for f in range(frames_ref.shape[0]):
        limit = limit + jnp.where(first <= row_pos, frames_ref[f], 0)
        first = first + frames_ref[f]
    bias[...] = jnp.where(key_pos < limit, 0.0, -1e30)
    kvbuf[own] = kv_ref[...]

    pl.semaphore_wait(barrier, n * H - 1)

    def hop(src, buf, send, recv, side, zs, cs, g):
        target = ({"seq": jnp.minimum(z + 1, S - 1)}, {"seq": jnp.maximum(z - 1, 0)}, {"sub": (c + 1) % C})[side]
        index = zs * C + cs
        return pltpu.make_async_remote_copy(
            src_ref=src if src is not None else buf.at[index, g],
            dst_ref=buf.at[index, g],
            send_sem=send.at[side, zs, g],
            recv_sem=recv.at[index, g],
            device_id=target,
            device_id_type=MESH,
        )

    def launch(src, buf, send, recv, g):
        @pl.when(z + 1 < S)
        def _():
            hop(src, buf, send, recv, 0, z, c, g).start()

        @pl.when(z > 0)
        def _():
            hop(src, buf, send, recv, 1, z, c, g).start()

        if C > 1:
            hop(src, buf, send, recv, 2, z, c, g).start()

    def relay(buf, send, recv, d, g):
        @pl.when(z - d >= 0)
        def _():
            hop(None, buf, send, recv, 0, z - d, c, g).wait_recv()

            @pl.when(z + 1 < S)
            def _():
                hop(None, buf, send, recv, 0, z - d, c, g).start()

            if C > 1:
                hop(None, buf, send, recv, 2, z - d, c, g).start()

        @pl.when(z + d < S)
        def _():
            hop(None, buf, send, recv, 1, z + d, c, g).wait_recv()

            @pl.when(z > 0)
            def _():
                hop(None, buf, send, recv, 1, z + d, c, g).start()

            if C > 1:
                hop(None, buf, send, recv, 2, z + d, c, g).start()

    def from_partner(buf, send, recv, zs, g):
        if C > 1:
            hop(None, buf, send, recv, 2, zs, (c + 1) % C, g).wait_recv()

    def drain(src, buf, send, recv, zs, g):
        @pl.when((zs <= z) & (z + 1 < S))
        def _():
            hop(src, buf, send, recv, 0, zs, c, g).wait_send()

        @pl.when((zs >= z) & (z > 0))
        def _():
            hop(src, buf, send, recv, 1, zs, c, g).wait_send()

        if C > 1:
            hop(src, buf, send, recv, 2, zs, c, g).wait_send()

    for g in range(G):
        launch(kv_ref.at[g], kvbuf, kv_send, kv_recv, g)

    def kv_gather(g):
        lax.fori_loop(1, S, lambda d, x: (relay(kvbuf, kv_send, kv_recv, d, g), x)[1], 0)
        lax.fori_loop(0, S, lambda s, x: (from_partner(kvbuf, kv_send, kv_recv, s, g), x)[1], 0)

    factor = HEAD_WIDTH ** (-0.5) * math.log2(math.e)
    heads_each = width // HEAD_WIDTH
    pack = 2 if heads_each % 2 == 0 else 1
    span = pack * HEAD_WIDTH

    def attention(g):
        key = kvbuf[:, g, 0].reshape(total, HEAD_WIDTH)
        value = kvbuf[:, g, 1].reshape(total, HEAD_WIDTH)

        def few_heads(b, carry):
            at = pl.multiple_of(g * width + b * span, span)
            q = q_ref[:, pl.ds(at, span)]
            q = jnp.concatenate(
                [q[:, k * HEAD_WIDTH:(k + 1) * HEAD_WIDTH] for k in range(pack)], axis=0
            )
            s = lax.dot_general(q, key, (((1,), (1,)), ((), ())), preferred_element_type=jnp.float32)
            s = (s.reshape(pack, rows, total) + bias[...][None]).reshape(pack * rows, total)
            top = jnp.max(s, axis=-1, keepdims=True)
            w = jnp.exp2((s - top) * factor)
            amount = jnp.sum(w, axis=-1, keepdims=True)
            o = jnp.dot(w.astype(jnp.bfloat16), value, preferred_element_type=jnp.float32)
            o = (o / amount).astype(jnp.bfloat16)
            o = jnp.concatenate([o[k * rows:(k + 1) * rows] for k in range(pack)], axis=1)
            att_out[:, pl.ds(at, span)] = o
            attbuf[own, g, :, pl.ds(pl.multiple_of(b * span, span), span)] = o
            return carry

        lax.fori_loop(0, heads_each // pack, few_heads, 0)

    def result_copy(index):
        return pltpu.make_async_remote_copy(
            src_ref=pbuf.at[index],
            dst_ref=retbuf.at[h, home_slot],
            send_sem=ret_send.at[index],
            recv_sem=ret_recv.at[h, home_slot],
            device_id={"seq": index // C, "sub": index % C, "heads": home},
            device_id_type=MESH,
        )

    def multiply(zb, g, last):
        a = attbuf[pl.ds(zb * C, C), g].reshape(C * rows, width)
        w = proj[pl.ds(pl.multiple_of(g * width, width), width), :]
        at = pl.ds(pl.multiple_of(zb * C * rows, C * rows), C * rows)
        summed = acc[at, :] + jnp.dot(a, w, preferred_element_type=jnp.float32)
        if not last:
            acc[at, :] = summed
            return
        summed = summed.astype(jnp.bfloat16)
        for k in range(C):
            index = zb * C + k
            pbuf[index] = summed[k * rows:(k + 1) * rows]
            here = (index == own) & (home == h)

            @pl.when(here)
            def _():
                retbuf[h, home_slot] = summed[k * rows:(k + 1) * rows]

            @pl.when(jnp.logical_not(here))
            def _():
                result_copy(index).start()

    def process(g, last):
        from_partner(attbuf, at_send, at_recv, z, g)
        multiply(z, g, last)

        def step(d, carry):
            relay(attbuf, at_send, at_recv, d, g)

            @pl.when(z - d >= 0)
            def _():
                from_partner(attbuf, at_send, at_recv, z - d, g)
                multiply(z - d, g, last)

            @pl.when(z + d < S)
            def _():
                from_partner(attbuf, at_send, at_recv, z + d, g)
                multiply(z + d, g, last)

            return carry

        lax.fori_loop(1, S, step, 0)

    acc[...] = jnp.zeros_like(acc)
    lax.fori_loop(0, G, lambda g, x: (kv_gather(g), x)[1], 0)

    def head_step(g, carry):
        attention(g)
        launch(None, attbuf, at_send, at_recv, g)

        @pl.when(g == 0)
        def _():
            proj_copy.wait()

        @pl.when(g > 0)
        def _():
            process(g - 1, False)

        return carry

    lax.fori_loop(0, G, head_step, 0)
    process(G - 1, True)

    squares = jnp.zeros((rows, 1), jnp.float32)
    for b in range(blocks):
        where = slice(b * cols, (b + 1) * cols)
        value = res_ref[:, where].astype(jnp.float32)
        for k in range(H):
            @pl.when(jnp.logical_not((home == h) & (home_slot == b) & (k == h)))
            def _():
                pltpu.make_async_remote_copy(
                    src_ref=pbuf.at[0], dst_ref=retbuf.at[k, b],
                    send_sem=ret_send.at[0], recv_sem=ret_recv.at[k, b],
                    device_id={"heads": home}, device_id_type=MESH,
                ).wait_recv()
            value = value + retbuf[k, b].astype(jnp.float32)
        hidden = value.astype(jnp.bfloat16)
        hidden_out[:, where] = hidden
        wide = hidden.astype(jnp.float32)
        squares = squares + jnp.sum(wide * wide, axis=-1, keepdims=True)

    ebuf[h] = jnp.broadcast_to(squares, (rows, 128))

    def share(k, side):
        other = (h + k) % H if side == 0 else (h + H - k) % H
        return pltpu.make_async_remote_copy(
            src_ref=ebuf.at[h], dst_ref=ebuf.at[h if side == 0 else other],
            send_sem=en_send.at[k], recv_sem=en_recv.at[h if side == 0 else other],
            device_id={"heads": (h + k) % H}, device_id_type=MESH,
        )

    for k in range(1, H):
        share(k, 0).start()
    for k in range(1, H):
        share(k, 1).wait_recv()
    energy = ebuf[0]
    for k in range(1, H):
        energy = energy + ebuf[k]
    inverse = lax.rsqrt(energy[:, 0:1] / (H * res_ref.shape[1]) + 1e-06)
    for b in range(blocks):
        where = slice(b * cols, (b + 1) * cols)
        normed_out[:, where] = (
            hidden_out[:, where].astype(jnp.float32) * inverse * gain_ref[:, where]
        ).astype(jnp.bfloat16)

    for k in range(1, H):
        share(k, 0).wait_send()

    def finish(i, carry):
        zs, g = i // G, i % G
        drain(kv_ref.at[g], kvbuf, kv_send, kv_recv, zs, g)
        drain(None, attbuf, at_send, at_recv, zs, g)
        return carry

    lax.fori_loop(0, S * G, finish, 0)

    def finish_results(index, carry):
        @pl.when(jnp.logical_not((index == own) & (home == h)))
        def _():
            result_copy(index).wait_send()
        return carry

    lax.fori_loop(0, n, finish_results, 0)


def shards(dims, queries, keys, values, half_order, frame_lengths, out_proj, residual_in, norm_gain):
    S, C, H = dims
    n = S * C
    rows = queries.shape[0]
    G = keys.shape[1] // HEAD_WIDTH
    width = queries.shape[1] // G
    cols = out_proj.shape[1]
    kv = jnp.stack(
        [jnp.transpose(a.reshape(rows, G, HEAD_WIDTH), (1, 0, 2)) for a in (keys, values)], axis=1
    )
    vmem = pl.BlockSpec(memory_space=pltpu.VMEM)
    smem = pl.BlockSpec(memory_space=pltpu.SMEM)
    dma = pltpu.SemaphoreType.DMA
    bf16, f32 = jnp.bfloat16, jnp.float32
    return pl.pallas_call(
        functools.partial(kernel, (S, C, H, G)),
        out_shape=(
            jax.ShapeDtypeStruct(queries.shape, bf16),
            jax.ShapeDtypeStruct(residual_in.shape, bf16),
            jax.ShapeDtypeStruct(residual_in.shape, bf16),
        ),
        in_specs=[smem, smem, vmem, vmem, pl.BlockSpec(memory_space=pl.ANY), vmem, vmem],
        out_specs=(vmem, vmem, vmem),
        scratch_shapes=[
            pltpu.VMEM((n, G, 2, rows, HEAD_WIDTH), bf16),
            pltpu.VMEM((n, G, rows, width), bf16),
            pltpu.VMEM(out_proj.shape, bf16),
            pltpu.VMEM((rows, n * rows), f32),
            pltpu.VMEM((n * rows, cols), f32),
            pltpu.VMEM((n, rows, cols), bf16),
            pltpu.VMEM((H, n // H, rows, cols), bf16),
            pltpu.VMEM((H, rows, 128), f32),
            dma(()),
            dma((3, S, G)),
            dma((n, G)),
            dma((3, S, G)),
            dma((n, G)),
            dma((n,)),
            dma((H, n // H)),
            dma((H,)),
            dma((H,)),
        ],
        compiler_params=pltpu.CompilerParams(
            collective_id=0, has_side_effects=True, vmem_limit_bytes=60 * 1024 * 1024
        ),
    )(half_order, frame_lengths, queries, kv, out_proj, residual_in, norm_gain[None, :])


def solution(mesh):
    dims = (mesh.shape["seq"], mesh.shape["sub"], mesh.shape["heads"])
    token = P(("groups", "seq", "sub"), "heads")
    in_specs = (
        token, token, token, P("groups"), P("groups"),
        P("heads", ("seq", "sub")), token, P("heads"),
    )
    return jax.shard_map(
        functools.partial(shards, dims), mesh=mesh, in_specs=in_specs,
        out_specs=(token, token, token), check_vma=False,
    )
```

time: 243 us -> 143 us (0.59)
  waiting for transfers between devices: 145 us -> 0 us
  Pallas kernels: 0 us -> 133 us
  blocking collectives: 32 us -> 0 us
  matrix products: 25.3 us -> 0 us
  other arithmetic: 16.2 us -> 0.73 us
  between operations: 15.1 us -> 0.66 us
    pallas_call x0 -> x1, Pallas kernels: none -> 133 us  [shards(): pl.pallas_call(functools.partial(kernel, (S, C, H, G)), out_shape=(jax.Sh...]
    all_gather x3 -> x0, waiting for transfers between devices: 124 us -> none  [the longest x1 81.7 us: shards(): gathered = lax.all_gather(attended, ('seq', 'sub'), axis=0, tiled=True)]
    all_to_all x1 -> x0, blocking collectives: 28.2 us -> none  [shards(): lax.all_to_all(column_terms.astype(jnp.bfloat16), ('seq', 'sub'), split_a...]
    dot_general x3 -> x0, matrix products: 25.3 us -> none  [the longest x1 9.06 us: shards(): jnp.dot(gathered, out_proj, preferred_element_type=jnp.float32)]
    reduce_scatter x1 -> x0, waiting for transfers between devices: 19.6 us -> none  [shards(): lax.psum_scatter(head_terms, 'heads', scatter_dimension=1, tiled=True)]
    reduce_sum x5 -> x0, other arithmetic: 11.5 us -> none  [the longest x1 7.98 us: absorb_piece(): denominator = jnp.sum(weights, axis=-1)]
    unnamed x7 -> x5, local copies, waits for them, and re-layouts: 1.43 us -> 8.09 us
    psum x1 -> x0, blocking collectives: 3.78 us -> none  [shards(): energy = lax.psum(jnp.sum(widened * widened, axis=1), 'heads') / OUT_WIDTH]
  transfers between devices with their start and end apart: 4 -> 0, of which waited for: 4 -> 0; matrix products, arithmetic and copies ran while one was open for 2% -> 0% of each run, Pallas kernels for 0% -> 0%
where the time goes in v2:
time: 143 us
  Pallas kernels  133 us (93%)
  local copies, waits for them, and re-layouts  8.36 us (6%)
    pallas_call x1, Pallas kernels, shards(): pl.pallas_call(functools.partial(kernel, (S, C, H, G)), out_shape=(jax.Sh...  133 us
    unnamed x5, local copies, waits for them, and re-layouts  8.09 us

profile of v2, /device:TPU:1, one launch (start us, length us, event | category | flops | bytes accessed | tf_op | source)
XLA Modules:
  0.0 143.0 jit_solution(5755278073549162352)
XLA Ops:
  0.6 1.0 copy.11
  1.7 0.1 copy.12
  1.8 1.0 copy.13
  2.8 0.1 copy.14
  3.0 0.7 pad_maximum_fusion.kv_ref
  3.7 133.3 %shard_map.103 = (bf16[128,4096]{1,0:T(8,128)(2,1)}, bf16[128,2048]{1,0:T(8,128)(2,1)}, bf16[128,2048]{1,0:T(8,128)(2,1)}) custom-call(s32[16]{0:T(128)} %order_ref.1, s32[8]{0:T(128)} %frames_ref.1, bf16[128,4096]{1,0:T(8,128)(2,1)} %q_ref.1, bf16[4,2,128,128]{3,2,1,0:T(8,128)(2,1)} %pad_maximum_fusion.kv_ref, bf16[4096,512]{1,0:T(8,128)(2,1)} %proj_hbm.1, ...), custom_call_target="tpu_custom_call" | custom-call | tf_op jit(solution)/shard_map/pallas_call | solution.py:318
  137.0 2.3 %copy.18 = bf16[128,4096]{1,0:T(8,128)(2,1)} copy(bf16[128,4096]{1,0:T(8,128)(2,1)} %get-tuple-element.6) | data formatting | bytes 2097152
  139.3 1.9 %copy.19 = bf16[128,2048]{1,0:T(8,128)(2,1)} copy(bf16[128,2048]{1,0:T(8,128)(2,1)} %get-tuple-element.7) | data formatting | bytes 1048576
  141.2 1.9 %copy.20 = bf16[128,2048]{1,0:T(8,128)(2,1)} copy(bf16[128,2048]{1,0:T(8,128)(2,1)} %get-tuple-element.8) | data formatting | bytes 1048576

commit v3 on v2

--- a/solution.py
+++ b/solution.py
@@ -12,9 +12,9 @@
 MESH = pl.DeviceIdType.MESH
 
 
-def kernel(dims, order_ref, frames_ref, q_ref, kv_ref, proj_hbm, res_ref, gain_ref,
+def kernel(dims, order_ref, frames_ref, q_ref, keys_ref, values_ref, proj_hbm, res_ref, gain_ref,
            att_out, hidden_out, normed_out,
-           kvbuf, attbuf, proj, bias, acc, pbuf, retbuf, ebuf,
+           kvbuf, attbuf, proj, bias, pbuf, retbuf, ebuf,
            proj_sem, kv_send, kv_recv, at_send, at_recv, ret_send, ret_recv, en_send, en_recv):
     S, C, H, G = dims
     n = S * C
@@ -63,15 +63,18 @@
         limit = limit + jnp.where(first <= row_pos, frames_ref[f], 0)
         first = first + frames_ref[f]
     bias[...] = jnp.where(key_pos < limit, 0.0, -1e30)
-    kvbuf[own] = kv_ref[...]
+    for g in range(G):
+        part = slice(g * HEAD_WIDTH, (g + 1) * HEAD_WIDTH)
+        kvbuf[own, g, 0] = keys_ref[:, part]
+        kvbuf[own, g, 1] = values_ref[:, part]
 
     pl.semaphore_wait(barrier, n * H - 1)
 
-    def hop(src, buf, send, recv, side, zs, cs, g):
+    def hop(buf, send, recv, side, zs, cs, g):
         target = ({"seq": jnp.minimum(z + 1, S - 1)}, {"seq": jnp.maximum(z - 1, 0)}, {"sub": (c + 1) % C})[side]
         index = zs * C + cs
         return pltpu.make_async_remote_copy(
-            src_ref=src if src is not None else buf.at[index, g],
+            src_ref=buf.at[index, g],
             dst_ref=buf.at[index, g],
             send_sem=send.at[side, zs, g],
             recv_sem=recv.at[index, g],
@@ -79,62 +82,65 @@
             device_id_type=MESH,
         )
 
-    def launch(src, buf, send, recv, g):
+    def launch(buf, send, recv, g):
         @pl.when(z + 1 < S)
         def _():
-            hop(src, buf, send, recv, 0, z, c, g).start()
+            hop(buf, send, recv, 0, z, c, g).start()
 
         @pl.when(z > 0)
         def _():
-            hop(src, buf, send, recv, 1, z, c, g).start()
+            hop(buf, send, recv, 1, z, c, g).start()
 
         if C > 1:
-            hop(src, buf, send, recv, 2, z, c, g).start()
+            hop(buf, send, recv, 2, z, c, g).start()
 
     def relay(buf, send, recv, d, g):
         @pl.when(z - d >= 0)
         def _():
-            hop(None, buf, send, recv, 0, z - d, c, g).wait_recv()
+            hop(buf, send, recv, 0, z - d, c, g).wait_recv()
 
             @pl.when(z + 1 < S)
             def _():
-                hop(None, buf, send, recv, 0, z - d, c, g).start()
+                hop(buf, send, recv, 0, z - d, c, g).start()
 
             if C > 1:
-                hop(None, buf, send, recv, 2, z - d, c, g).start()
+                hop(buf, send, recv, 2, z - d, c, g).start()
 
         @pl.when(z + d < S)
         def _():
-            hop(None, buf, send, recv, 1, z + d, c, g).wait_recv()
+            hop(buf, send, recv, 1, z + d, c, g).wait_recv()
 
             @pl.when(z > 0)
             def _():
-                hop(None, buf, send, recv, 1, z + d, c, g).start()
+                hop(buf, send, recv, 1, z + d, c, g).start()
 
             if C > 1:
-                hop(None, buf, send, recv, 2, z + d, c, g).start()
+                hop(buf, send, recv, 2, z + d, c, g).start()
 
     def from_partner(buf, send, recv, zs, g):
         if C > 1:
-            hop(None, buf, send, recv, 2, zs, (c + 1) % C, g).wait_recv()
-
-    def drain(src, buf, send, recv, zs, g):
+            hop(buf, send, recv, 2, zs, (c + 1) % C, g).wait_recv()
+
+    def drain(buf, send, recv, zs, g):
         @pl.when((zs <= z) & (z + 1 < S))
         def _():
-            hop(src, buf, send, recv, 0, zs, c, g).wait_send()
+            hop(buf, send, recv, 0, zs, c, g).wait_send()
 
         @pl.when((zs >= z) & (z > 0))
         def _():
-            hop(src, buf, send, recv, 1, zs, c, g).wait_send()
+            hop(buf, send, recv, 1, zs, c, g).wait_send()
 
         if C > 1:
-            hop(src, buf, send, recv, 2, zs, c, g).wait_send()
-
-    for g in range(G):
-        launch(kv_ref.at[g], kvbuf, kv_send, kv_recv, g)
-
-    def kv_gather(g):
+            hop(buf, send, recv, 2, zs, c, g).wait_send()
+
+    def kv_relay(g):
+        @pl.when(g + 1 < G)
+        def _():
+            launch(kvbuf, kv_send, kv_recv, g + 1)
+
         lax.fori_loop(1, S, lambda d, x: (relay(kvbuf, kv_send, kv_recv, d, g), x)[1], 0)
+
+    def kv_partner(g):
         lax.fori_loop(0, S, lambda s, x: (from_partner(kvbuf, kv_send, kv_recv, s, g), x)[1], 0)
 
     factor = HEAD_WIDTH ** (-0.5) * math.log2(math.e)
@@ -143,6 +149,7 @@
     span = pack * HEAD_WIDTH
 
     def attention(g):
+        kv_partner(g)
         key = kvbuf[:, g, 0].reshape(total, HEAD_WIDTH)
         value = kvbuf[:, g, 1].reshape(total, HEAD_WIDTH)
 
@@ -162,9 +169,18 @@
             o = jnp.concatenate([o[k * rows:(k + 1) * rows] for k in range(pack)], axis=1)
             att_out[:, pl.ds(at, span)] = o
             attbuf[own, g, :, pl.ds(pl.multiple_of(b * span, span), span)] = o
+
+            @pl.when((g == 0) & (b + 1 < G))
+            def _():
+                kv_relay(jnp.minimum(b + 1, G - 1))
+
             return carry
 
         lax.fori_loop(0, heads_each // pack, few_heads, 0)
+
+        @pl.when(g == 0)
+        def _():
+            lax.fori_loop(min(heads_each // pack + 1, G), G, lambda k, x: (kv_relay(k), x)[1], 0)
 
     def result_copy(index):
         return pltpu.make_async_remote_copy(
@@ -176,14 +192,15 @@
             device_id_type=MESH,
         )
 
-    def multiply(zb, g, last):
-        a = attbuf[pl.ds(zb * C, C), g].reshape(C * rows, width)
-        w = proj[pl.ds(pl.multiple_of(g * width, width), width), :]
-        at = pl.ds(pl.multiple_of(zb * C * rows, C * rows), C * rows)
-        summed = acc[at, :] + jnp.dot(a, w, preferred_element_type=jnp.float32)
-        if not last:
-            acc[at, :] = summed
-            return
+    def multiply(zb):
+        summed = jnp.zeros((C * rows, cols), jnp.float32)
+        for g in range(G):
+            from_partner(attbuf, at_send, at_recv, zb, g)
+            summed = summed + jnp.dot(
+                attbuf[pl.ds(zb * C, C), g].reshape(C * rows, width),
+                proj[g * width:(g + 1) * width, :],
+                preferred_element_type=jnp.float32,
+            )
         summed = summed.astype(jnp.bfloat16)
         for k in range(C):
             index = zb * C + k
@@ -198,46 +215,32 @@
             def _():
                 result_copy(index).start()
 
-    def process(g, last):
-        from_partner(attbuf, at_send, at_recv, z, g)
-        multiply(z, g, last)
-
-        def step(d, carry):
-            relay(attbuf, at_send, at_recv, d, g)
-
-            @pl.when(z - d >= 0)
-            def _():
-                from_partner(attbuf, at_send, at_recv, z - d, g)
-                multiply(z - d, g, last)
-
-            @pl.when(z + d < S)
-            def _():
-                from_partner(attbuf, at_send, at_recv, z + d, g)
-                multiply(z + d, g, last)
-
-            return carry
-
-        lax.fori_loop(1, S, step, 0)
-
-    acc[...] = jnp.zeros_like(acc)
-    lax.fori_loop(0, G, lambda g, x: (kv_gather(g), x)[1], 0)
+    launch(kvbuf, kv_send, kv_recv, 0)
+    kv_relay(jnp.int32(0))
 
     def head_step(g, carry):
         attention(g)
-        launch(None, attbuf, at_send, at_recv, g)
-
-        @pl.when(g == 0)
-        def _():
-            proj_copy.wait()
-
-        @pl.when(g > 0)
-        def _():
-            process(g - 1, False)
-
+        launch(attbuf, at_send, at_recv, g)
         return carry
 
     lax.fori_loop(0, G, head_step, 0)
-    process(G - 1, True)
+    proj_copy.wait()
+    multiply(z)
+
+    def step(d, carry):
+        lax.fori_loop(0, G, lambda g, x: (relay(attbuf, at_send, at_recv, d, g), x)[1], 0)
+
+        @pl.when(z - d >= 0)
+        def _():
+            multiply(z - d)
+
+        @pl.when(z + d < S)
+        def _():
+            multiply(z + d)
+
+        return carry
+
+    lax.fori_loop(1, S, step, 0)
 
     squares = jnp.zeros((rows, 1), jnp.float32)
     for b in range(blocks):
@@ -286,8 +289,8 @@
 
     def finish(i, carry):
         zs, g = i // G, i % G
-        drain(kv_ref.at[g], kvbuf, kv_send, kv_recv, zs, g)
-        drain(None, attbuf, at_send, at_recv, zs, g)
+        drain(kvbuf, kv_send, kv_recv, zs, g)
+        drain(attbuf, at_send, at_recv, zs, g)
         return carry
 
     lax.fori_loop(0, S * G, finish, 0)
@@ -308,9 +311,6 @@
     G = keys.shape[1] // HEAD_WIDTH
     width = queries.shape[1] // G
     cols = out_proj.shape[1]
-    kv = jnp.stack(
-        [jnp.transpose(a.reshape(rows, G, HEAD_WIDTH), (1, 0, 2)) for a in (keys, values)], axis=1
-    )
     vmem = pl.BlockSpec(memory_space=pltpu.VMEM)
     smem = pl.BlockSpec(memory_space=pltpu.SMEM)
     dma = pltpu.SemaphoreType.DMA
@@ -322,14 +322,13 @@
             jax.ShapeDtypeStruct(residual_in.shape, bf16),
             jax.ShapeDtypeStruct(residual_in.shape, bf16),
         ),
-        in_specs=[smem, smem, vmem, vmem, pl.BlockSpec(memory_space=pl.ANY), vmem, vmem],
+        in_specs=[smem, smem, vmem, vmem, vmem, pl.BlockSpec(memory_space=pl.ANY), vmem, vmem],
         out_specs=(vmem, vmem, vmem),
         scratch_shapes=[
             pltpu.VMEM((n, G, 2, rows, HEAD_WIDTH), bf16),
             pltpu.VMEM((n, G, rows, width), bf16),
             pltpu.VMEM(out_proj.shape, bf16),
             pltpu.VMEM((rows, n * rows), f32),
-            pltpu.VMEM((n * rows, cols), f32),
             pltpu.VMEM((n, rows, cols), bf16),
             pltpu.VMEM((H, n // H, rows, cols), bf16),
             pltpu.VMEM((H, rows, 128), f32),
@@ -344,9 +343,9 @@
             dma((H,)),
         ],
         compiler_params=pltpu.CompilerParams(
-            collective_id=0, has_side_effects=True, vmem_limit_bytes=60 * 1024 * 1024
+            collective_id=0, has_side_effects=True, vmem_limit_bytes=40 * 1024 * 1024
         ),
-    )(half_order, frame_lengths, queries, kv, out_proj, residual_in, norm_gain[None, :])
+    )(half_order, frame_lengths, queries, keys, values, out_proj, residual_in, norm_gain[None, :])
 
 
 def solution(mesh):

time: 143 us -> 137 us (0.958)
  Pallas kernels: 133 us -> 126 us
  local copies, waits for them, and re-layouts: 8.36 us -> 10.8 us
    pallas_call x1, Pallas kernels: 133 us -> 126 us  [shards(): pl.pallas_call(functools.partial(kernel, (S, C, H, G)), out_shape=(jax.Sh...]
    unnamed x5 -> x19, local copies, waits for them, and re-layouts: 8.09 us -> 10.8 us
where the time goes in v3:
time: 137 us
  Pallas kernels  126 us (92%)
  local copies, waits for them, and re-layouts  10.8 us (8%)
    pallas_call x1, Pallas kernels, shards(): pl.pallas_call(functools.partial(kernel, (S, C, H, G)), out_shape=(jax.Sh...  126 us
    unnamed x19, local copies, waits for them, and re-layouts  10.8 us

profile of v3, /device:TPU:1, one launch (start us, length us, event | category | flops | bytes accessed | tf_op | source)
XLA Modules:
  0.0 137.1 jit_solution(8853419559476077575)
XLA Ops:
  0.6 0.0 copy-start
  0.6 2.2 %copy-done = bf16[4096,512]{1,0:T(8,128)(2,1)S(1)} copy-done((bf16[4096,512]{1,0:T(8,128)(2,1)S(1)}, bf16[4096,512]{1,0:T(8,128)(2,1)}, u32[]{:S(2)}) %copy-start) | copy-done | bytes 4194328
  2.8 0.0 copy-start.1
  2.8 1.2 copy-done.1
  4.0 0.0 copy-start.2
  4.0 1.0 copy-done.2
  5.1 0.0 copy-start.3
  5.1 0.9 copy-done.3
  6.0 0.0 copy-start.4
  6.0 0.9 copy-done.4
  6.9 0.0 copy-start.5
  6.9 0.7 copy-done.5
  7.6 0.0 copy-start.6
  7.6 0.7 copy-done.6
  8.3 0.0 copy-start.7
  8.3 0.7 copy-done.7
  8.9 125.6 %shard_map.103 = (bf16[128,4096]{1,0:T(8,128)(2,1)S(1)}, bf16[128,2048]{1,0:T(8,128)(2,1)S(1)}, bf16[128,2048]{1,0:T(8,128)(2,1)S(1)}) custom-call(s32[16]{0:T(128)S(1)} %copy-done.6, s32[8]{0:T(128)S(1)} %copy-done.7, bf16[128,4096]{1,0:T(8,128)(2,1)S(1)} %copy-done.1, bf16[128,512]{1,0:T(8,128)(2,1)S(1)} %copy-done.3, bf16[128,512]{1,0:T(8,128)(2,1)S(1)} %copy-done.4, ...), custom_call_target="tpu_custom_call" | custom-call | tf_op jit(solution)/shard_map/pallas_call | solution.py:318
  134.6 1.0 copy.14
  135.5 0.8 copy.15
  136.3 0.8 copy.16
Async XLA Ops:
  0.6 2.2 %copy-start = (bf16[4096,512]{1,0:T(8,128)(2,1)S(1)}, bf16[4096,512]{1,0:T(8,128)(2,1)}, u32[]{:S(2)}) copy-start(bf16[4096,512]{1,0:T(8,128)(2,1)} %proj_hbm.1) | copy-start | bytes 12582916
  2.8 1.2 copy-start.1
  4.0 1.0 copy-start.2
  5.1 0.9 copy-start.3
  6.0 0.9 copy-start.4
  6.9 0.7 copy-start.5
  7.6 0.7 copy-start.6
  8.3 0.7 copy-start.7

commit v4 on v3

--- a/solution.py
+++ b/solution.py
@@ -12,10 +12,10 @@
 MESH = pl.DeviceIdType.MESH
 
 
-def kernel(dims, order_ref, frames_ref, q_ref, keys_ref, values_ref, proj_hbm, res_ref, gain_ref,
+def kernel(dims, order_ref, frames_ref, q_hbm, keys_ref, values_ref, proj_hbm, res_hbm, gain_ref,
            att_out, hidden_out, normed_out,
-           kvbuf, attbuf, proj, bias, pbuf, retbuf, ebuf,
-           proj_sem, kv_send, kv_recv, at_send, at_recv, ret_send, ret_recv, en_send, en_recv):
+           kvbuf, attbuf, proj, q_ref, res_ref, bias, pbuf, retbuf, ebuf,
+           in_sem, kv_send, kv_recv, at_send, at_recv, ret_send, ret_recv, en_send, en_recv):
     S, C, H, G = dims
     n = S * C
     blocks = n // H
@@ -28,8 +28,12 @@
     home = own // blocks
     home_slot = own % blocks
 
-    proj_copy = pltpu.make_async_copy(proj_hbm, proj, proj_sem)
+    q_copy = pltpu.make_async_copy(q_hbm, q_ref, in_sem.at[0])
+    q_copy.start()
+    proj_copy = pltpu.make_async_copy(proj_hbm, proj, in_sem.at[1])
     proj_copy.start()
+    res_copy = pltpu.make_async_copy(res_hbm, res_ref, in_sem.at[2])
+    res_copy.start()
 
     barrier = pltpu.get_barrier_semaphore()
 
@@ -217,6 +221,7 @@
 
     launch(kvbuf, kv_send, kv_recv, 0)
     kv_relay(jnp.int32(0))
+    q_copy.wait()
 
     def head_step(g, carry):
         attention(g)
@@ -242,6 +247,7 @@
 
     lax.fori_loop(1, S, step, 0)
 
+    res_copy.wait()
     squares = jnp.zeros((rows, 1), jnp.float32)
     for b in range(blocks):
         where = slice(b * cols, (b + 1) * cols)
@@ -311,6 +317,7 @@
     G = keys.shape[1] // HEAD_WIDTH
     width = queries.shape[1] // G
     cols = out_proj.shape[1]
+    hbm = pl.BlockSpec(memory_space=pltpu.HBM)
     vmem = pl.BlockSpec(memory_space=pltpu.VMEM)
     smem = pl.BlockSpec(memory_space=pltpu.SMEM)
     dma = pltpu.SemaphoreType.DMA
@@ -322,17 +329,19 @@
             jax.ShapeDtypeStruct(residual_in.shape, bf16),
             jax.ShapeDtypeStruct(residual_in.shape, bf16),
         ),
-        in_specs=[smem, smem, vmem, vmem, vmem, pl.BlockSpec(memory_space=pl.ANY), vmem, vmem],
+        in_specs=[smem, smem, hbm, vmem, vmem, hbm, hbm, vmem],
         out_specs=(vmem, vmem, vmem),
         scratch_shapes=[
             pltpu.VMEM((n, G, 2, rows, HEAD_WIDTH), bf16),
             pltpu.VMEM((n, G, rows, width), bf16),
             pltpu.VMEM(out_proj.shape, bf16),
+            pltpu.VMEM(queries.shape, bf16),
+            pltpu.VMEM(residual_in.shape, bf16),
             pltpu.VMEM((rows, n * rows), f32),
             pltpu.VMEM((n, rows, cols), bf16),
             pltpu.VMEM((H, n // H, rows, cols), bf16),
             pltpu.VMEM((H, rows, 128), f32),
-            dma(()),
+            dma((3,)),
             dma((3, S, G)),
             dma((n, G)),
             dma((3, S, G)),
@@ -343,7 +352,7 @@
             dma((H,)),
         ],
         compiler_params=pltpu.CompilerParams(
-            collective_id=0, has_side_effects=True, vmem_limit_bytes=40 * 1024 * 1024
+            collective_id=0, has_side_effects=True, vmem_limit_bytes=51 * 1024 * 1024
         ),
     )(half_order, frame_lengths, queries, keys, values, out_proj, residual_in, norm_gain[None, :])
 

time: 137 us -> 134 us (0.978)
  local copies, waits for them, and re-layouts: 10.8 us -> 7.41 us
    unnamed x19 -> x15, local copies, waits for them, and re-layouts: 10.8 us -> 7.41 us
where the time goes in v4:
time: 134 us; the launch traced here: 133 us
  Pallas kernels  125 us (93%)
  local copies, waits for them, and re-layouts  7.41 us (6%)
    pallas_call x1, Pallas kernels, shards(): pl.pallas_call(functools.partial(kernel, (S, C, H, G)), out_shape=(jax.Sh...  125 us
    unnamed x15, local copies, waits for them, and re-layouts  7.41 us

profile of v4, /device:TPU:1, one launch (start us, length us, event | category | flops | bytes accessed | tf_op | source)
XLA Modules:
  0.0 133.5 jit_solution(2300080142788512269)
XLA Ops:
  0.6 0.0 copy-start
  0.6 1.0 copy-done
  1.7 0.0 copy-start.1
  1.7 0.9 copy-done.1
  2.6 0.0 copy-start.2
  2.6 0.9 copy-done.2
  3.5 0.0 copy-start.3
  3.5 0.7 copy-done.3
  4.2 0.0 copy-start.4
  4.2 0.7 copy-done.4
  4.8 0.0 copy-start.5
  4.8 0.7 copy-done.5
  5.5 125.4 %shard_map.103 = (bf16[128,4096]{1,0:T(8,128)(2,1)S(1)}, bf16[128,2048]{1,0:T(8,128)(2,1)S(1)}, bf16[128,2048]{1,0:T(8,128)(2,1)S(1)}) custom-call(s32[16]{0:T(128)S(1)} %copy-done.4, s32[8]{0:T(128)S(1)} %copy-done.5, bf16[128,4096]{1,0:T(8,128)(2,1)} %q_hbm.1, bf16[128,512]{1,0:T(8,128)(2,1)S(1)} %copy-done.1, bf16[128,512]{1,0:T(8,128)(2,1)S(1)} %copy-done.2, ...), custom_call_target="tpu_custom_call" | custom-call | tf_op jit(solution)/shard_map/pallas_call | solution.py:325
  130.9 1.0 copy.14
  131.9 0.8 copy.15
  132.7 0.8 copy.16
Async XLA Ops:
  0.6 1.0 copy-start
  1.7 0.9 copy-start.1
  2.6 0.9 copy-start.2
  3.5 0.7 copy-start.3
  4.2 0.7 copy-start.4
  4.8 0.7 copy-start.5
